TPU v7x, 32 devices: a 4x4x1 block of a 4x4x8 slice. The times are simulated.
32 devices in a mesh: rep: 2 (over z, core), dp: 16 (over x, y).
Axes of the slice: x: 4, y: 4, z: 1, core: 2. Of those that a mesh axis runs over, the one named last changes fastest.
The devices are a block of a 4x4x8 slice.
Arguments:
- x: bfloat16 [32, 1024, 512], P(('rep', 'dp')), parts along dimension 0
- dy: bfloat16 [32, 1024, 512], P(('rep', 'dp')), parts along dimension 0
- w_gate: bfloat16 [2, 512, 8192], P(None, 'dp')
- w_up: bfloat16 [2, 512, 8192], P(None, 'dp')
- w_down: bfloat16 [2, 8192, 512], P(None, 'dp')
Outputs:
- output 1: bfloat16 [32, 1024, 512], P(('rep', 'dp')), parts along dimension 0
- output 2: bfloat16 [4, 512, 8192], P('rep', 'dp'), parts along dimension 0
- output 3: bfloat16 [4, 512, 8192], P('rep', 'dp'), parts along dimension 0
- output 4: bfloat16 [4, 8192, 512], P('rep', 'dp'), parts along dimension 0
There are 2 independent parts. A program takes and returns all parts, laid end to end along the dimension named above; an argument that names none is the same for every part.
All inputs are finite; a program needn't handle non-finite values.
Results may differ from a plain program's by a relative error of at most 0.018.
Values are sent between devices in bfloat16 or wider.
A program may use at most 768 MiB of HBM per device.

v0:
```python
import jax
import jax.numpy as jnp
from jax import lax

NAMES = ("w_gate", "w_up", "w_down")


def matmul(a, w):
    return jnp.dot(a, w, preferred_element_type=jnp.float32).astype(jnp.bfloat16)


def normed(h):
    wide = h.astype(jnp.float32)
    scale = lax.rsqrt(jnp.mean(wide**2, -1, keepdims=True) + 1e-6)
    return (wide * scale).astype(jnp.bfloat16)


def layer(h, w):
    a = normed(h)
    gate = jnp.dot(a, w["w_gate"], preferred_element_type=jnp.float32)
    up = jnp.dot(a, w["w_up"], preferred_element_type=jnp.float32)
    return h + matmul((jax.nn.silu(gate) * up).astype(jnp.bfloat16), w["w_down"])


def stack(weights, h):
    for number in range(weights["w_gate"].shape[0]):
        h = layer(h, {name: w[number] for name, w in weights.items()})
    return h


def solution(mesh):
    groups = mesh.shape["rep"]

    def step(x, dy, *weights):
        shape = x.shape
        x, dy = (t.reshape(groups, -1, *t.shape[1:]) for t in (x, dy))

        def of_a_group(x, dy):
            _, back = jax.vjp(stack, dict(zip(NAMES, weights, strict=True)), x)
            by_weights, by_x = back(dy)
            return (by_x, *(by_weights[name] for name in NAMES))

        by_x, *by_weights = jax.vmap(of_a_group)(x, dy)
        return (by_x.reshape(shape), *(t.reshape(-1, *t.shape[2:]) for t in by_weights))

    return step
```

profile of v0, /device:TPU:97, one launch (start us, length us, event | category | flops | bytes accessed | tf_op | source)
XLA Modules:
  0.0 1170.1 jit_solution(10877533186954238638)
XLA Ops:
  22.3 56.8 %all-gather.30.cloned.1.call-done = bf16[1,512,8192]{2,1,0:T(8,128)(2,1)} async-done(((bf16[1,32,8192]{2,1,0:T(8,128)(2,1)}), bf16[1,512,8192]{2,1,0:T(8,128)(2,1)}) %all-gather.30.cloned.1.call-update) | async-done | bytes 8388624 | tf_op jit(solution)/vmap(jvp())/squeeze | solution.py:27
  79.1 19.0 %fusion.57 = f32[1024,8192]{1,0:T(8,128)} fusion(bf16[1,512,8192]{2,1,0:T(8,128)(2,1)} %all-gather.30.cloned.1.call-done, bf16[1,1024,512]{2,1,0:T(8,128)(2,1)} %param.1, f32[1024]{0:T(1024)S(1)} %get-tuple-element.13), kind=kOutput, calls=%fused_computation.65 | convolution fusion | flops 8591507456 | bytes 42995712 | tf_op jit(solution)/vmap(jvp())/dot_general | solution.py:20
  98.2 48.6 %all-gather.32.cloned.1.call-done = bf16[1,512,8192]{2,1,0:T(8,128)(2,1)} async-done(((bf16[1,32,8192]{2,1,0:T(8,128)(2,1)}), bf16[1,512,8192]{2,1,0:T(8,128)(2,1)}) %all-gather.32.cloned.1.call-update) | async-done | bytes 8388624 | tf_op jit(solution)/vmap(jvp())/squeeze | solution.py:27
  146.8 17.9 %fusion.53 = f32[1024,8192]{1,0:T(8,128)} fusion(bf16[1,512,8192]{2,1,0:T(8,128)(2,1)} %all-gather.32.cloned.1.call-done, bf16[1,1024,512]{2,1,0:T(8,128)(2,1)S(1)} %copy-done.4, f32[1024]{0:T(1024)S(1)} %get-tuple-element.13), kind=kOutput, calls=%fused_computation.61 | convolution fusion | flops 8591507456 | bytes 42995712 | tf_op jit(solution)/vmap(jvp())/dot_general | solution.py:21
  164.7 27.4 %fusion.24 = bf16[1024,8192]{1,0:T(8,128)(2,1)} fusion(f32[1024,8192]{1,0:T(8,128)} %fusion.53, f32[1024,8192]{1,0:T(8,128)} %fusion.57), kind=kLoop, calls=%fused_computation.34 | loop fusion | flops 50331648 | bytes 83886080
  192.1 21.8 %all-gather.34.cloned.1.call-done = bf16[1,8192,512]{2,1,0:T(8,128)(2,1)} async-done(((bf16[1,512,512]{2,1,0:T(8,128)(2,1)}), bf16[1,8192,512]{2,1,0:T(8,128)(2,1)}) %all-gather.34.cloned.1.call-update) | async-done | bytes 8388624 | tf_op jit(solution)/vmap(jvp())/squeeze | solution.py:27
  228.9 52.0 %all-gather.36.cloned.1.call-done = bf16[1,512,8192]{2,1,0:T(8,128)(2,1)} async-done(((bf16[1,32,8192]{2,1,0:T(8,128)(2,1)}), bf16[1,512,8192]{2,1,0:T(8,128)(2,1)}) %all-gather.36.cloned.1.call-update) | async-done | bytes 8388624 | tf_op jit(solution)/vmap(jvp())/squeeze | solution.py:27
  280.8 19.0 %fusion.47 = f32[1024,8192]{1,0:T(8,128)} fusion(bf16[1,512,8192]{2,1,0:T(8,128)(2,1)} %all-gather.36.cloned.1.call-done, bf16[1,1,1024,512]{2,3,1,0:T(8,128)(2,1)S(1)} %get-tuple-element.15, f32[1024]{0:T(1024)S(1)} %bitcast.320), kind=kOutput, calls=%fused_computation.55 | convolution fusion | flops 8591507456 | bytes 42995712 | tf_op jit(solution)/vmap(jvp())/dot_general | solution.py:20
  299.8 48.5 %all-gather.40.cloned.1.call-done = bf16[1,512,8192]{2,1,0:T(8,128)(2,1)} async-done(((bf16[1,32,8192]{2,1,0:T(8,128)(2,1)}), bf16[1,512,8192]{2,1,0:T(8,128)(2,1)}) %all-gather.40.cloned.1.call-update) | async-done | bytes 8388624 | tf_op jit(solution)/vmap(jvp())/squeeze | solution.py:27
  348.4 18.7 %fusion.41 = f32[1024,8192]{1,0:T(8,128)} fusion(bf16[1,512,8192]{2,1,0:T(8,128)(2,1)} %all-gather.40.cloned.1.call-done, bf16[1,1,1024,512]{2,3,1,0:T(8,128)(2,1)S(1)} %get-tuple-element.15, f32[1024]{0:T(1024)S(1)} %bitcast.321), kind=kOutput, calls=%fused_computation.49 | convolution fusion | flops 8591507456 | bytes 42995712 | tf_op jit(solution)/vmap(jvp())/dot_general | solution.py:21
  367.1 48.3 %all-gather.38.cloned.1.call-done = bf16[1,8192,512]{2,1,0:T(8,128)(2,1)} async-done(((bf16[1,512,512]{2,1,0:T(8,128)(2,1)}), bf16[1,8192,512]{2,1,0:T(8,128)(2,1)}) %all-gather.38.cloned.1.call-update) | async-done | bytes 8388624 | tf_op jit(solution)/vmap(jvp())/squeeze | solution.py:27
  430.5 27.2 %fusion.4 = bf16[1024,8192]{1,0:T(8,128)(2,1)S(1)} fusion(f32[1024,8192]{1,0:T(8,128)} %fusion.47, f32[1024,8192]{1,0:T(8,128)} %fusion.41, bf16[1024,8192]{1,0:T(8,128)(2,1)} %convolution_convert_fusion.1), kind=kLoop, calls=%fused_computation.10 | loop fusion | flops 100663296 | bytes 100663296
  475.7 22.4 %fusion.69 = (f32[1024]{0:T(1024)S(1)}, bf16[1,1,1024,512]{2,3,1,0:T(8,128)(2,1)S(1)}) fusion(bf16[1,1,1024,512]{2,3,1,0:T(8,128)(2,1)S(1)} %get-tuple-element.15, bf16[1024,512]{0,1:T(8,128)(2,1)S(1)} %fusion.76, bf16[1,512,8192]{2,1,0:T(8,128)(2,1)} %all-gather.40.cloned.1.call-done, bf16[1024,8192]{1,0:T(8,128)(2,1)} %convolution_convert_fusion.1, ...), kind=kOutput, calls=%fused_computation.88 | convolution fusion | flops 8643410944 | bytes 61870080 | tf_op jit(solution)/vmap(transpose(jvp()))/dot_general | solution.py:21
  498.8 16.2 %convolution_bitcast_fusion = f32[1,8192,512]{2,1,0:T(8,128)} fusion(bf16[1024,8192]{1,0:T(8,128)(2,1)} %fusion.24, bf16[1,1,1024,512]{2,3,1,0:T(8,128)(2,1)S(1)} %fusion.119), kind=kOutput, calls=%fused_computation.46 | convolution fusion | flops 8589934592 | bytes 34603008 | tf_op jit(solution)/vmap(transpose(jvp()))/dot_general | solution.py:9
  515.2 29.5 %fusion.32 = f32[1,8192,512]{2,1,0:T(8,128)} fusion(f32[1024,8192]{1,0:T(8,128)} %fusion.41, f32[1024,8192]{1,0:T(8,128)} %fusion.47, bf16[1,1024,512]{2,1,0:T(8,128)(2,1)S(1)} %copy-done.12), kind=kOutput, calls=%fused_computation.43 | convolution fusion | flops 8640266240 | bytes 84934656 | tf_op jit(solution)/vmap(transpose(jvp()))/dot_general | solution.py:9
  544.8 25.6 %fusion.35 = f32[1,512,8192]{2,1,0:T(8,128)} fusion(bf16[1024,8192]{1,0:T(8,128)(2,1)} %convolution_convert_fusion.1, f32[1024,8192]{1,0:T(8,128)} %fusion.47, bf16[1,1,1024,512]{2,3,1,0:T(8,128)(2,1)S(1)} %get-tuple-element.15, f32[1024]{0:T(1024)S(1)} %bitcast.323), kind=kOutput, calls=%fused_computation.44 | convolution fusion | flops 8641839104 | bytes 68161536 | tf_op jit(solution)/vmap(transpose(jvp()))/dot_general | solution.py:21
  570.5 16.1 %convolution_convert_fusion = bf16[1024,8192]{1,0:T(8,128)(2,1)} fusion(bf16[1,8192,512]{2,1,0:T(8,128)(2,1)} %all-gather.34.cloned.1.call-done, bf16[1,1,1024,512]{2,3,1,0:T(8,128)(2,1)S(1)} %fusion.119), kind=kOutput, calls=%fused_computation.41 | convolution fusion | flops 8598323200 | bytes 26214400 | tf_op jit(solution)/vmap(transpose(jvp()))/dot_general | solution.py:9
  586.6 27.1 %fusion.7 = bf16[1024,8192]{1,0:T(8,128)(2,1)S(1)} fusion(f32[1024,8192]{1,0:T(8,128)} %fusion.57, f32[1024,8192]{1,0:T(8,128)} %fusion.53, bf16[1024,8192]{1,0:T(8,128)(2,1)} %convolution_convert_fusion), kind=kLoop, calls=%fused_computation.13 | loop fusion | flops 100663296 | bytes 100663296
  631.9 22.1 %fusion.65 = (f32[1024]{0:T(1024)S(1)}, bf16[1,1,1024,512]{2,3,1,0:T(8,128)(2,1)}) fusion(bf16[1,1024,512]{1,2,0:T(8,128)(2,1)S(1)} %copy-done.6, bf16[1024,512]{0,1:T(8,128)(2,1)S(1)} %fusion.70, bf16[1,512,8192]{2,1,0:T(8,128)(2,1)} %all-gather.32.cloned.1.call-done, bf16[1024,8192]{1,0:T(8,128)(2,1)} %convolution_convert_fusion, f32[1024,8192]{1,0:T(8,128)} %fusion.57), kind=kOutput, calls=%fused_computation.84 | convolution fusion | flops 8643410944 | bytes 61870080 | tf_op jit(solution)/vmap(transpose(jvp()))/dot_general | solution.py:21
  654.0 25.6 %fusion.38 = f32[1,512,8192]{2,1,0:T(8,128)} fusion(bf16[1024,8192]{1,0:T(8,128)(2,1)} %convolution_convert_fusion, f32[1024,8192]{1,0:T(8,128)} %fusion.57, bf16[1,1024,512]{1,2,0:T(8,128)(2,1)S(1)} %copy-done.6, f32[1024]{0:T(1024)S(1)} %bitcast.329), kind=kOutput, calls=%fused_computation.45 | convolution fusion | flops 8641839104 | bytes 68161536 | tf_op jit(solution)/vmap(transpose(jvp()))/dot_general | solution.py:21
  730.4 105.8 %reduce-scatter.23.cloned.1.call-done = f32[1,32,8192]{2,1,0:T(8,128)} async-done(((f32[1,512,8192]{2,1,0:T(8,128)}), f32[1,32,8192]{2,1,0:T(8,128)}) %reduce-scatter.23.cloned.1.call-update) | async-done | bytes 1048592
  837.5 106.7 %reduce-scatter.25.cloned.1.call-done = f32[1,32,8192]{2,1,0:T(8,128)} async-done(((f32[1,512,8192]{2,1,0:T(8,128)}), f32[1,32,8192]{2,1,0:T(8,128)}) %reduce-scatter.25.cloned.1.call-update) | async-done | bytes 1048592
  946.6 105.9 %reduce-scatter.19.cloned.1.call-done = f32[1,32,8192]{2,1,0:T(8,128)} async-done(((f32[1,512,8192]{2,1,0:T(8,128)}), f32[1,32,8192]{2,1,0:T(8,128)}) %reduce-scatter.19.cloned.1.call-update) | async-done | bytes 1048592
  1053.7 106.8 %reduce-scatter.21.cloned.1.call-done = f32[1,32,8192]{2,1,0:T(8,128)} async-done(((f32[1,512,8192]{2,1,0:T(8,128)}), f32[1,32,8192]{2,1,0:T(8,128)}) %reduce-scatter.21.cloned.1.call-update) | async-done | bytes 1048592
  (83 shorter events, 140.3 us)
Async XLA Ops:
  7.2 71.9 %all-gather.30.cloned.1.call-start = ((), (), s32[]{:S(2)}) async-start(), calls=%async_computation.6 | async-start | bytes 8912896 | tf_op jit(solution)/vmap(jvp())/squeeze | solution.py:27
  9.6 137.2 %all-gather.32.cloned.1.call-start = ((), (), s32[]{:S(2)}) async-start(), calls=%async_computation.7 | async-start | bytes 8912896 | tf_op jit(solution)/vmap(jvp())/squeeze | solution.py:27
  12.0 201.9 %all-gather.34.cloned.1.call-start = ((), (), s32[]{:S(2)}) async-start(), calls=%async_computation.8 | async-start | bytes 8912896 | tf_op jit(solution)/vmap(jvp())/squeeze | solution.py:27
  14.4 266.4 %all-gather.36.cloned.1.call-start = ((), (), s32[]{:S(2)}) async-start(), calls=%async_computation.9 | async-start | bytes 8912896 | tf_op jit(solution)/vmap(jvp())/squeeze | solution.py:27
  15.0 333.3 %all-gather.40.cloned.1.call-start = ((), (), s32[]{:S(2)}) async-start(), calls=%async_computation.11 | async-start | bytes 8912896 | tf_op jit(solution)/vmap(jvp())/squeeze | solution.py:27
  15.7 399.6 %all-gather.38.cloned.1.call-start = ((), (), s32[]{:S(2)}) async-start(), calls=%async_computation.10 | async-start | bytes 8912896 | tf_op jit(solution)/vmap(jvp())/squeeze | solution.py:27
  16.3 700.7 %reduce-scatter.29.cloned.1.call-start = ((), (), s32[]{:S(2)}) async-start(), calls=%async_computation.17 | async-start | bytes 17825792
  19.4 194.5 %copy-start.5 = (bf16[1,1024,512]{1,2,0:T(8,128)(2,1)}, bf16[1,1024,512]{1,2,0:T(8,128)(2,1)S(1)}, u32[]{:S(2)}) copy-start(bf16[1,1024,512]{1,2,0:T(8,128)(2,1)S(1)} %copy.1) | copy-start | bytes 3145732
  79.1 67.7 %copy-start.4 = (bf16[1,1024,512]{2,1,0:T(8,128)(2,1)S(1)}, bf16[1,1024,512]{2,1,0:T(8,128)(2,1)}, u32[]{:S(2)}) copy-start(bf16[1,1024,512]{2,1,0:T(8,128)(2,1)} %param.1) | copy-start | bytes 3145732
  228.8 315.9 %copy-start.2 = (bf16[1,1,1024,512]{2,3,1,0:T(8,128)(2,1)}, bf16[1,1,1024,512]{2,3,1,0:T(8,128)(2,1)S(1)}, u32[]{:S(2)}) copy-start(bf16[1,1,1024,512]{2,3,1,0:T(8,128)(2,1)S(1)} %get-tuple-element.15) | copy-start | bytes 3145732
  228.9 315.9 %copy-start.10 = (f32[1,1,1024]{2,1,0:T(1,128)}, f32[1,1,1024]{2,1,0:T(1,128)S(1)}, u32[]{:S(2)}) copy-start(f32[1,1,1024]{2,1,0:T(1,128)S(1)} %rsqrt.23) | copy-start | bytes 12292
  299.8 115.5 %copy-start.12 = (bf16[1,1024,512]{2,1,0:T(8,128)(2,1)S(1)}, bf16[1,1024,512]{2,1,0:T(8,128)(2,1)}, u32[]{:S(2)}) copy-start(bf16[1,1024,512]{2,1,0:T(8,128)(2,1)} %param) | copy-start | bytes 3145732
  457.7 5.7 copy-start
  475.7 22.4 %copy-start.7 = (bf16[1,1024,512]{1,2,0:T(8,128)(2,1)S(1)}, bf16[1,1024,512]{1,2,0:T(8,128)(2,1)}, u32[]{:S(2)}) copy-start(bf16[1,1024,512]{1,2,0:T(8,128)(2,1)} %copy) | copy-start | bytes 3145732
  498.8 71.7 %copy-start.8 = (bf16[1,1,1024,512]{2,3,1,0:T(8,128)(2,1)}, bf16[1,1,1024,512]{2,3,1,0:T(8,128)(2,1)S(1)}, u32[]{:S(2)}) copy-start(bf16[1,1,1024,512]{2,3,1,0:T(8,128)(2,1)S(1)} %fusion.119) | copy-start | bytes 3145732
  515.1 213.0 %reduce-scatter.27.cloned.1.call-start = ((), (), s32[]{:S(2)}) async-start(), calls=%async_computation.16 | async-start | bytes 17825792
  544.7 291.5 %reduce-scatter.23.cloned.1.call-start = ((), (), s32[]{:S(2)}) async-start(), calls=%async_computation.14 | async-start | bytes 17825792
  570.5 373.8 %reduce-scatter.25.cloned.1.call-start = ((), (), s32[]{:S(2)}) async-start(), calls=%async_computation.15 | async-start | bytes 17825792
  613.7 5.7 copy-start.1
  619.5 12.4 %copy-start.6 = (bf16[1,1024,512]{1,2,0:T(8,128)(2,1)S(1)}, bf16[1,1024,512]{1,2,0:T(8,128)(2,1)}, u32[]{:S(2)}) copy-start(bf16[1,1024,512]{1,2,0:T(8,128)(2,1)} %copy-done.5) | copy-start | bytes 3145732
  631.8 22.1 %copy-start.13 = (f32[1024]{0:T(1024)S(1)}, f32[1024]{0:T(1024)}, u32[]{:S(2)}) copy-start(f32[1024]{0:T(1024)} %get-tuple-element.12) | copy-start | bytes 12292
  679.6 1.2 copy-start.11
  679.6 372.8 %reduce-scatter.19.cloned.1.call-start = ((), (), s32[]{:S(2)}) async-start(), calls=%async_computation.12 | async-start | bytes 17825792
  696.6 463.9 %reduce-scatter.21.cloned.1.call-start = ((), (), s32[]{:S(2)}) async-start(), calls=%async_computation.13 | async-start | bytes 17825792
  (2 other events, 2.5 us)
Sparse Core Ops, SparseCore 0:
  10.0 69.1 all-gather.29
  81.6 65.0 all-gather.31
  148.8 65.0 all-gather.33
  215.7 65.0 all-gather.35
  283.2 65.0 all-gather.39
  350.2 65.0 all-gather.37
  515.2 104.6 reduce-scatter.28
  623.1 104.9 reduce-scatter.26
  731.3 104.8 reduce-scatter.22
  839.3 104.8 reduce-scatter.24
  947.5 104.9 reduce-scatter.18
  1055.5 104.9 reduce-scatter.20
where the time goes:
time: 1180 us; the launch traced here: 1170 us
  waiting for transfers between devices  713 us (60%)
  matrix products  318 us (27%)
  other arithmetic  97.3 us (8%)
  local copies, waits for them, and re-layouts  25.6 us (2%)
  between operations  14.9 us (1%)
    unnamed x18, waiting for transfers between devices  437 us
    squeeze x6, waiting for transfers between devices, stack(): h = layer(h, {name: w[number] for name, w in weights.items()})  276 us
    dot_general x6, matrix products, layer(): up = jnp.dot(a, w['w_up'], preferred_element_type=jnp.float32)  132 us
    dot_general x6, matrix products, layer(): gate = jnp.dot(a, w['w_gate'], preferred_element_type=jnp.float32)  94.3 us
    dot_general x5, matrix products, matmul(): jnp.dot(a, w, preferred_element_type=jnp.float32).astype(jnp.bfloat16)  91.9 us
    unnamed x3, other arithmetic  81.7 us
  transfers between devices with their start and end apart: 12, of which 11 were waited for; matrix products, arithmetic and copies ran while one was open for 28% of the time, Pallas kernels for 0%

commit v1 on v0

v1 whole, which is shorter than its diff:
```python
import functools
import math

import jax
import jax.numpy as jnp
from jax import lax
from jax.experimental import pallas as pl
from jax.experimental.pallas import tpu as pltpu
from jax.sharding import PartitionSpec as P

F32, BF16 = jnp.float32, jnp.bfloat16
MESH = pl.DeviceIdType.MESH
LANES, PIECE = 128, 32
PER = LANES // PIECE
NN, NT, TN = ((1,), (0,)), ((1,), (1,)), ((0,), (0,))
SIGNS = (1, -1)
VMEM_LIMIT = 62 * 1024 * 1024


def dot(a, b, dims=NN):
    return lax.dot_general(a, b, (dims, ((), ())), preferred_element_type=F32)


def scale_of(wide):
    return lax.rsqrt(jnp.mean(wide**2, -1, keepdims=True) + 1e-6)


def place(n):
    side = math.isqrt(n)
    me = lax.axis_index("dp")
    x, y = me // side, me % side

    def at(v, u, w):
        u, w = lax.rem(u + 2 * side, side), lax.rem(w + 2 * side, side)
        return u * side + w if v == 0 else w * side + u

    return me, side, ((x, y), (y, x)), at


def entry_barrier(n, partner=None):
    me, side, uw, at = place(n)
    barrier = pltpu.get_barrier_semaphore()
    (u, w), others = uw[0], 4
    for s in SIGNS:
        pl.semaphore_signal(barrier, inc=1, device_id={"dp": at(0, u + s, w)}, device_id_type=MESH)
        pl.semaphore_signal(barrier, inc=1, device_id={"dp": at(0, u, w + s)}, device_id_type=MESH)
    if partner is not None:
        pl.semaphore_signal(barrier, inc=1, device_id={"rep": partner}, device_id_type=MESH)
        others += 1
    return lambda: pl.semaphore_wait(barrier, others)


def regroup(pieces, lane):
    for k in range(PER):
        out = pieces[k]
        for q in range(PER):
            if q != k:
                out = jnp.where(lane == q, pltpu.roll(pieces[q], (PIECE * (q - k)) % LANES, 1), out)
        yield k, out


def gather_kernel(n, tile, x_ref, wg_ref, wu_ref, wd_ref, g_ref, h_ref, own, a_ref, acc, w_buf, send_sem, recv_sem, pair_send, pair_recv, own_sem, load_sem):
    layers, chunks = g_ref.shape[:2]
    height, width = own.shape[3:]
    depth = width
    tokens = x_ref.shape[0]
    me, side, uw, at = place(n)
    rep = lax.axis_index("rep")
    core = lax.rem(rep, 2)
    partner = rep + 1 - 2 * core
    half = chunks // 2
    units = layers * half
    entered = entry_barrier(n, partner)

    first = pl.multiple_of(core * height, height)
    lane = lax.broadcasted_iota(jnp.int32, (height, LANES), 1) // PIECE
    per_device = wg_ref.shape[2] // n
    tiles, groups = per_device // LANES, n // PER

    def fill(i, _):
        layer, rest = i // (tiles * groups), lax.rem(i, tiles * groups)
        t, u = rest // groups, lax.rem(rest, groups)
        for m, w in enumerate((wg_ref, wu_ref)):
            pieces = [
                w[layer, pl.ds(first, height), pl.ds(pl.multiple_of((PER * u + q) * per_device + t * LANES, LANES), LANES)].astype(F32)
                for q in range(PER)
            ]
            for k, out in regroup(pieces, lane):
                own[layer, PER * t + k, m, :, pl.ds(pl.multiple_of(u * LANES, LANES), LANES)] = out.astype(BF16)
        return 0

    def fill_down(i, _):
        layer, j = i // chunks, lax.rem(i, chunks)
        own[layer, j, 2] = wd_ref[layer, pl.ds(pl.multiple_of(j * 2 * height + first, height), height), :]
        return 0

    lax.fori_loop(0, layers * tiles * groups, fill, 0)
    lax.fori_loop(0, layers * chunks, fill_down, 0)
    keep = [pltpu.make_async_copy(own.at[layer], g_ref.at[layer, :, me, core], own_sem.at[layer]) for layer in range(layers)]
    for copy in keep:
        copy.start()
    entered()

    def norm(i, _):
        rows = pl.ds(pl.multiple_of(i * tile, tile), tile)
        wide = x_ref[rows].astype(F32)
        a_ref[rows] = (wide * scale_of(wide)).astype(BF16)
        acc[rows] = jnp.zeros((tile, depth), F32)
        return 0

    def place_of(k, v):
        return k // half, 2 * lax.rem(k, half) + v

    def block(k, v, d):
        layer, j = place_of(k, v)
        return g_ref.at[layer, j, d, core]

    def copy_to(k, v, d, device, src=None):
        return pltpu.make_async_remote_copy(
            src_ref=block(k, v, d) if src is None else src,
            dst_ref=block(k, v, d),
            send_sem=send_sem,
            recv_sem=recv_sem.at[k, v, d],
            device_id={"dp": device},
            device_id_type=MESH,
        )

    def await_block(k, v, d):
        copy_to(k, v, d, me).wait_recv()

    def begin(k):
        for v, (u, w) in enumerate(uw):
            layer, j = place_of(k, v)
            for s in SIGNS:
                copy_to(k, v, me, at(v, u + s, w), own.at[layer, j]).start()
                copy_to(k, v, me, at(v, u, w + s), own.at[layer, j]).start()

    def spread(k, v, d, u, w):
        for s in SIGNS:
            copy_to(k, v, d, at(v, u, w + s)).start()

    def pass_on(k, v, column, sign):
        u, w = uw[v]
        for s in SIGNS:
            await_block(k, v, at(v, u + column, w + s))
        copy_to(k, v, at(v, u + column, w - sign), at(v, u, w + sign)).start()

    def near(k):
        sign = 1 - 2 * lax.rem(k, 2)
        for v, (u, w) in enumerate(uw):
            for s in SIGNS:
                await_block(k, v, at(v, u + s, w))
            copy_to(k, v, at(v, u - sign, w), at(v, u + sign, w)).start()
            for s in SIGNS:
                spread(k, v, at(v, u + s, w), u, w)
            pass_on(k, v, 0, sign)

    def middle(k):
        sign = 1 - 2 * lax.rem(k, 2)
        for v, (u, w) in enumerate(uw):
            await_block(k, v, at(v, u + 2, w))
            spread(k, v, at(v, u + 2, w), u, w)
            pass_on(k, v, 1, -sign)
            pass_on(k, v, -1, sign)

    def far(k):
        sign = 1 - 2 * lax.rem(k, 2)
        for v, (u, w) in enumerate(uw):
            pass_on(k, v, 2, -sign)
            await_block(k, v, at(v, u, w + 2))

    def pair_copy(k):
        layer, j = place_of(k, 0)
        ref = g_ref.at[layer, pl.ds(j, 2), :, core]
        return pltpu.make_async_remote_copy(
            src_ref=ref, dst_ref=ref, send_sem=pair_send, recv_sem=pair_recv.at[k], device_id={"rep": partner}, device_id_type=MESH
        )

    def last(k):
        for v, (u, w) in enumerate(uw):
            for column in (1, -1, 2):
                await_block(k, v, at(v, u + column, w + 2))
        pair_copy(k).start()

    def load(k, v):
        layer, j = place_of(k, v)
        slot = 2 * lax.rem(k, 2) + v
        return pltpu.make_async_copy(g_ref.at[layer, j], w_buf.at[slot], load_sem.at[slot])

    def both(k):
        layer, j = place_of(k, 0)
        ref = g_ref.at[layer, pl.ds(j, 2), :, 1 - core]
        pltpu.make_async_remote_copy(
            src_ref=ref, dst_ref=ref, send_sem=pair_send, recv_sem=pair_recv.at[k], device_id={"rep": partner}, device_id_type=MESH
        ).wait_recv()

        @pl.when(k < half)
        def _():
            for v in range(2):
                load(k, v).start()

    def forward(k):
        for v in range(2):
            load(k, v).wait()
            slot = 2 * lax.rem(k, 2) + v

            def rows_of(i, _):
                rows = pl.ds(pl.multiple_of(i * tile, tile), tile)
                a = a_ref[rows]
                gate = dot(a, w_buf[slot, :, :, 0].reshape(depth, width))
                up = dot(a, w_buf[slot, :, :, 1].reshape(depth, width))
                hidden = (gate * jax.nn.sigmoid(gate) * up).astype(BF16)
                acc[rows] += dot(hidden, w_buf[slot, :, :, 2].reshape(width, depth))
                return 0

            lax.fori_loop(0, tokens // tile, rows_of, 0)

    def step(t, _):
        @pl.when(t < units)
        def _():
            begin(t)

        @pl.when(t == 0)
        def _():
            lax.fori_loop(0, tokens // tile, norm, 0)

        @pl.when(t == 2)
        def _():
            for copy in keep:
                copy.wait()

        for lag, stage in ((4, last), (3, far), (2, middle), (1, near), (5, both)):

            @pl.when((t >= lag) & (t < units + lag))
            def _(lag=lag, stage=stage):
                stage(t - lag)

        @pl.when((t >= 6) & (t < half + 6))
        def _():
            forward(t - 6)

        return 0

    lax.fori_loop(0, units + 6, step, 0)

    def result(i, _):
        rows = pl.ds(pl.multiple_of(i * tile, tile), tile)
        h_ref[rows] = x_ref[rows] + acc[rows].astype(BF16)
        return 0

    lax.fori_loop(0, tokens // tile, result, 0)
    for sem, blocks in ((send_sem, n - 1), (pair_send, n)):
        ref = g_ref.at[:, :, pl.ds(0, blocks), 0]
        pltpu.make_async_copy(ref, ref, sem).wait()


def gather(n, x, wg, wu, wd):
    (layers, height, _), depth = wg.shape, x.shape[1]
    width = n * PIECE
    chunks = wd.shape[1] // PIECE
    assert depth == width and height == PIECE and layers == 2
    tile = min(256, x.shape[0])
    vmem = pl.BlockSpec(memory_space=pltpu.VMEM)
    return pl.pallas_call(
        functools.partial(gather_kernel, n, tile),
        out_shape=(
            jax.ShapeDtypeStruct((layers, chunks, n, 2, 3, height // 2, width), BF16),
            jax.ShapeDtypeStruct(x.shape, BF16),
        ),
        in_specs=[vmem] * 4,
        out_specs=(pl.BlockSpec(memory_space=pl.ANY), vmem),
        scratch_shapes=[
            pltpu.VMEM((layers, chunks, 3, height // 2, width), BF16),
            pltpu.VMEM(x.shape, BF16),
            pltpu.VMEM(x.shape, F32),
            pltpu.VMEM((4, n, 2, 3, height // 2, width), BF16),
            pltpu.SemaphoreType.DMA,
            pltpu.SemaphoreType.DMA((layers * chunks // 2, 2, n)),
            pltpu.SemaphoreType.DMA,
            pltpu.SemaphoreType.DMA((layers * chunks // 2,)),
            pltpu.SemaphoreType.DMA((layers,)),
            pltpu.SemaphoreType.DMA((4,)),
        ],
        compiler_params=pltpu.CompilerParams(collective_id=0, has_side_effects=True, vmem_limit_bytes=VMEM_LIMIT),
        name="gather_forward",
    )(x, wg, wu, wd)


def backward_kernel(
    n, tile, x_ref, h_ref, dy_ref, g_ref, o_ref, dx_ref,
    a_ref, at_ref, d_ref, hid_ref, dg_ref, du_ref, dag, dau, w_buf, terms, sums, out_buf,
    raw1_s, raw1_r, run1_s, run1_r, raw2_s, raw2_r, run2_s, run2_r,
    load_sem, out_sem, raw1_ss, raw1_rs, run1_ss, run1_rs, raw2_ss, raw2_rs, run2_ss, run2_rs,
):
    layers, chunks = g_ref.shape[:2]
    tokens, depth = x_ref.shape
    width = w_buf.shape[-1]
    height = terms.shape[3]
    low, part = height // 2, width // 2
    me, side, uw, at = place(n)
    total = layers * chunks
    entered = entry_barrier(n)

    def load(t):
        slot = lax.rem(t, 2)
        return pltpu.make_async_copy(g_ref.at[layers - 1 - t // chunks, lax.rem(t, chunks)], w_buf.at[slot], load_sem.at[slot])

    load(0).start()

    def row_tiles(body):
        def once(i, _):
            body(pl.ds(pl.multiple_of(i * tile, tile), tile))
            return 0

        lax.fori_loop(0, tokens // tile, once, 0)

    def start_layer(source):
        def body(rows):
            wide = source[rows].astype(F32)
            a = wide * scale_of(wide)
            a_ref[rows] = a.astype(BF16)
            at_ref[:, rows] = a.T.astype(BF16)
            dag[rows] = jnp.zeros((tile, depth), F32)
            dau[rows] = jnp.zeros((tile, depth), F32)

        row_tiles(body)

    def end_layer(source, target):
        def body(rows):
            wide = source[rows].astype(F32)
            scale = scale_of(wide)
            da = (dag[rows].astype(BF16) + dau[rows].astype(BF16)).astype(F32)
            inner = jnp.sum(da * wide, -1, keepdims=True)
            by_h = da * scale - wide * (scale * scale * scale * inner / depth)
            target[rows] = d_ref[rows] + by_h.astype(BF16)

        row_tiles(body)

    def compute(t):
        slot, held = lax.rem(t, 2), lax.rem(t, 3)
        load(t).wait()

        @pl.when(t + 1 < total)
        def _():
            load(t + 1).start()

        def body(rows):
            a, d = a_ref[rows], d_ref[rows]
            wg = w_buf[slot, :, :, 0].reshape(depth, width)
            wu = w_buf[slot, :, :, 1].reshape(depth, width)
            wd = w_buf[slot, :, :, 2].reshape(width, depth)
            gate, up = dot(a, wg), dot(a, wu)
            by_hid = dot(d, wd, NT).astype(BF16).astype(F32)
            sig = jax.nn.sigmoid(gate)
            silu = gate * sig
            dg = (by_hid * up * (sig + silu * (1 - sig))).astype(BF16)
            du = (by_hid * silu).astype(BF16)
            hid_ref[rows] = (silu * up).astype(BF16)
            dg_ref[rows] = dg
            du_ref[rows] = du
            dag[rows] += dot(dg, wg, NT)
            dau[rows] += dot(du, wu, NT)

        row_tiles(body)
        step = n // 2
        for m, (left, right, dims) in enumerate(((at_ref, dg_ref, NN), (at_ref, du_ref, NN), (hid_ref, d_ref, TN))):
            for i in range(2):
                some = pl.ds(i * step * height, step * height)
                value = dot(left[some] if dims is NN else left[:, some], right[...], dims)
                terms[held, m, i * step : (i + 1) * step] = value.reshape(step, height, width)

    def rows_of(v):
        return slice(v * low, (v + 1) * low)

    def cols_of(h):
        return slice(h * part, (h + 1) * part)

    flows = [(v, i, s) for v in range(2) for i, s in enumerate(SIGNS)]

    def send(k, v, i, second, src, dst, src_sem, dst_sem):
        u, w = uw[v]
        s = SIGNS[i]
        device = at(v, u, w + s) if second else at(v, u + s, w)
        return pltpu.make_async_remote_copy(
            src_ref=src.at[lax.rem(k, 2), v, i],
            dst_ref=dst.at[lax.rem(k, 4), v, i],
            send_sem=src_sem.at[lax.rem(k, 2), v, i],
            recv_sem=dst_sem.at[lax.rem(k, 4), v, i],
            device_id={"dp": device},
            device_id_type=MESH,
        )

    raw1 = lambda k, v, i: send(k, v, i, False, raw1_s, raw1_r, raw1_ss, raw1_rs)
    run1 = lambda k, v, i: send(k, v, i, False, run1_s, run1_r, run1_ss, run1_rs)
    raw2 = lambda k, v, i: send(k, v, i, True, raw2_s, raw2_r, raw2_ss, raw2_rs)
    run2 = lambda k, v, i: send(k, v, i, True, run2_s, run2_r, run2_ss, run2_rs)

    def wait_all(kind, k):
        for v, i, _ in flows:
            kind(k, v, i).wait()

    def start_all(kind, k):
        for v, i, _ in flows:
            kind(k, v, i).start()

    def pack(t):
        held, slot = lax.rem(t, 3), lax.rem(t, 2)
        for v, i, s in flows:
            u = uw[v][0]
            for w in range(side):
                raw1_s[slot, v, i, 0, w] = terms[held, :, at(v, u + 2, w), rows_of(v), cols_of(i)].astype(BF16)
                raw1_s[slot, v, i, 1, w] = terms[held, :, at(v, u + s, w), rows_of(v), cols_of(1 - i)].astype(BF16)

    def add1(k):
        held, slot, got = lax.rem(k, 3), lax.rem(k, 2), lax.rem(k, 4)
        wait_all(raw1, k)
        for v, i, s in flows:
            u = uw[v][0]
            for w in range(side):
                own = terms[held, :, at(v, u + s, w), rows_of(v), cols_of(i)]
                run1_s[slot, v, i, w] = (own + raw1_r[got, v, i, 0, w].astype(F32)).astype(BF16)
        start_all(run1, k)

    def turn(k):
        held, slot, got = lax.rem(k, 3), lax.rem(k, 2), lax.rem(k, 4)
        wait_all(run1, k)
        for v, i, s in flows:
            u = uw[v][0]
            for w in range(side):
                own = terms[held, :, at(v, u, w), rows_of(v), cols_of(i)]
                sums[slot, v, i, w] = own + run1_r[got, v, i, w].astype(F32) + raw1_r[got, v, 1 - i, 1, w].astype(F32)
        for v, i, s in flows:
            w = uw[v][1]
            raw2_s[slot, v, i, 0] = sums[slot, v, i, lax.rem(w + 2, side)].astype(BF16)
            raw2_s[slot, v, i, 1] = sums[slot, v, 1 - i, lax.rem(w + s + side, side)].astype(BF16)
        start_all(raw2, k)

    def add2(k):
        slot, got = lax.rem(k, 2), lax.rem(k, 4)
        wait_all(raw2, k)
        for v, i, s in flows:
            w = uw[v][1]
            own = sums[slot, v, i, lax.rem(w + s + side, side)]
            run2_s[slot, v, i] = (own + raw2_r[got, v, i, 0].astype(F32)).astype(BF16)
        start_all(run2, k)

    def put(k):
        slot = lax.rem(k, 2)
        return pltpu.make_async_copy(out_buf.at[slot], o_ref.at[layers - 1 - k // chunks, lax.rem(k, chunks)], out_sem.at[slot])

    def finish(k):
        slot, got = lax.rem(k, 2), lax.rem(k, 4)
        wait_all(run2, k)

        @pl.when(k >= 2)
        def _():
            put(k - 2).wait()

        for v, i, s in flows:
            w = uw[v][1]
            value = sums[slot, v, i, w] + run2_r[got, v, i].astype(F32) + raw2_r[got, v, 1 - i, 1].astype(F32)
            out_buf[slot, :, rows_of(v), cols_of(i)] = value.astype(BF16)
        put(k).start()

    def copy_d(rows):
        d_ref[rows] = dy_ref[rows]

    row_tiles(copy_d)
    start_layer(h_ref)
    entered()

    def step(t, _):
        for lag, stage in ((5, finish), (4, add2), (3, turn), (2, add1)):

            @pl.when((t >= lag) & (t < total + lag))
            def _(lag=lag, stage=stage):
                stage(t - lag)

        @pl.when(t == chunks)
        def _():
            end_layer(h_ref, d_ref)
            start_layer(x_ref)

        @pl.when(t < total)
        def _():
            compute(t)
            pack(t)
            start_all(raw1, t)

        @pl.when(t == total)
        def _():
            end_layer(x_ref, dx_ref)

        return 0

    lax.fori_loop(0, total + 6, step, 0)
    for k in (total - 2, total - 1):
        put(k).wait()


def backward(n, x, h, dy, g):
    layers, chunks, _, _, _, low, width = g.shape
    tokens, depth = x.shape
    side, part = math.isqrt(n), width // 2
    tile = min(256, tokens)
    vmem = pl.BlockSpec(memory_space=pltpu.VMEM)
    anywhere = pl.BlockSpec(memory_space=pl.ANY)
    pair = lambda count, *rest, dtype=BF16: pltpu.VMEM((count, 2, 2, *rest), dtype)
    sems = lambda count: pltpu.SemaphoreType.DMA((count, 2, 2))
    block = (3, low, part)
    return pl.pallas_call(
        functools.partial(backward_kernel, n, tile),
        out_shape=(
            jax.ShapeDtypeStruct((layers, chunks, 3, 2 * low, width), BF16),
            jax.ShapeDtypeStruct(x.shape, BF16),
        ),
        in_specs=[vmem, vmem, vmem, anywhere],
        out_specs=(anywhere, vmem),
        scratch_shapes=[
            pltpu.VMEM(x.shape, BF16),
            pltpu.VMEM(x.shape[::-1], BF16),
            pltpu.VMEM(x.shape, BF16),
            *[pltpu.VMEM((tokens, width), BF16)] * 3,
            *[pltpu.VMEM(x.shape, F32)] * 2,
            pltpu.VMEM((2, *g.shape[2:]), BF16),
            pltpu.VMEM((3, 3, n, 2 * low, width), F32),
            pair(2, side, *block, dtype=F32),
            pltpu.VMEM((2, 3, 2 * low, width), BF16),
            pair(2, 2, side, *block), pair(4, 2, side, *block),
            pair(2, side, *block), pair(4, side, *block),
            pair(2, 2, *block), pair(4, 2, *block),
            pair(2, *block), pair(4, *block),
            pltpu.SemaphoreType.DMA((2,)),
            pltpu.SemaphoreType.DMA((2,)),
            *[sems(2), sems(4)] * 4,
        ],
        compiler_params=pltpu.CompilerParams(collective_id=1, has_side_effects=True, vmem_limit_bytes=VMEM_LIMIT),
        name="backward_reduce",
    )(x, h, dy, g)


def restore_kernel(n, o_ref, dg_ref, du_ref):
    layers, chunks, _, height, width = o_ref.shape
    per_device = dg_ref.shape[2] // n
    tiles, groups = per_device // LANES, n // PER
    lane = lax.broadcasted_iota(jnp.int32, (height, LANES), 1) // PIECE

    def body(i, _):
        layer, rest = i // (tiles * groups), lax.rem(i, tiles * groups)
        t, u = rest // groups, lax.rem(rest, groups)
        for m, w in enumerate((dg_ref, du_ref)):
            pieces = [o_ref[layer, PER * t + k, m, :, pl.ds(pl.multiple_of(u * LANES, LANES), LANES)].astype(F32) for k in range(PER)]
            for q, out in regroup(pieces, lane):
                w[layer, :, pl.ds(pl.multiple_of((PER * u + q) * per_device + t * LANES, LANES), LANES)] = out.astype(BF16)
        return 0

    lax.fori_loop(0, layers * tiles * groups, body, 0)


def restore(n, o):
    layers, chunks, _, height, width = o.shape
    shape = jax.ShapeDtypeStruct((layers, height, chunks * width), BF16)
    vmem = pl.BlockSpec(memory_space=pltpu.VMEM)
    return pl.pallas_call(
        functools.partial(restore_kernel, n),
        out_shape=(shape, shape),
        in_specs=[vmem],
        out_specs=(vmem, vmem),
        compiler_params=pltpu.CompilerParams(vmem_limit_bytes=32 * 1024 * 1024),
        name="restore_order",
    )(o)


def solution(mesh):
    n = mesh.shape["dp"]

    def step(x, dy, wg, wu, wd):
        x, dy = x[0], dy[0]
        g, h = gather(n, x, wg, wu, wd)
        o, dx = backward(n, x, h, dy, g)
        dg, du = restore(n, o)
        return dx[None], dg, du, o[:, :, 2].reshape(wd.shape)

    tokens, rows, out = P(("rep", "dp"), None, None), P(None, "dp", None), P("rep", "dp", None)
    return jax.shard_map(step, mesh=mesh, in_specs=(tokens, tokens, rows, rows, rows), out_specs=(tokens, out, out, out), check_vma=False)
```

time: 1180 us -> 454 us (0.38)
  waiting for transfers between devices: 713 us -> 0 us
  Pallas kernels: 0 us -> 438 us
  matrix products: 318 us -> 0 us
  other arithmetic: 97.3 us -> 0 us
  local copies, waits for them, and re-layouts: 25.6 us -> 6.46 us
  between operations: 14.9 us -> 0.65 us
    pallas_call x0 -> x3, Pallas kernels: none -> 438 us  [the longest x1 277 us: backward(): pl.pallas_call(functools.partial(backward_kernel, n, tile), out_shape=(ja...]
    unnamed x18 -> x0, waiting for transfers between devices: 437 us -> none
    dot_general x17 -> x0, matrix products: 318 us -> none  [the longest x6 132 us: layer(): up = jnp.dot(a, w['w_up'], preferred_element_type=jnp.float32)]
    squeeze x6 -> x0, waiting for transfers between devices: 276 us -> none  [stack(): h = layer(h, {name: w[number] for name, w in weights.items()})]
    unnamed x3 -> x0, other arithmetic: 81.7 us -> none
    unnamed x31 -> x3, local copies, waits for them, and re-layouts: 18.8 us -> 4.15 us
  transfers between devices with their start and end apart: 12 -> 0, of which waited for: 11 -> 0; matrix products, arithmetic and copies ran while one was open for 28% -> 0% of each run, Pallas kernels for 0% -> 0%
where the time goes in v1:
time: 454 us; the launch traced here: 445 us
  Pallas kernels  438 us (96%)
  local copies, waits for them, and re-layouts  6.46 us (1%)
    pallas_call x1, Pallas kernels, backward(): pl.pallas_call(functools.partial(backward_kernel, n, tile), out_shape=(ja...  277 us
    pallas_call x1, Pallas kernels, gather(): pl.pallas_call(functools.partial(gather_kernel, n, tile), out_shape=(jax....  155 us

profile of v1, /device:TPU:97, one launch (start us, length us, event | category | flops | bytes accessed | tf_op | source)
XLA Modules:
  0.0 445.1 jit_solution(541889170784369952)
XLA Ops:
  0.6 155.5 %gather_forward.1 = (bf16[2,16,16,2,3,16,512]{6,5,4,3,2,1,0:T(8,128)(2,1)}, bf16[1024,512]{1,0:T(8,128)(2,1)}) custom-call(bf16[1024,512]{1,0:T(8,128)(2,1)} %bitcast.4, bf16[2,32,8192]{2,1,0:T(8,128)(2,1)} %wg_ref.1, bf16[2,32,8192]{2,1,0:T(8,128)(2,1)} %wu_ref.1, bf16[2,512,512]{2,1,0:T(8,128)(2,1)} %wd_ref.1), custom_call_target="tpu_custom_call" | custom-call | tf_op jit(solution)/shard_map/gather_forward/pallas_call | solution.py:264
  156.1 277.0 %backward_reduce.1 = (bf16[2,16,3,32,512]{4,3,2,1,0:T(8,128)(2,1)}, bf16[1024,512]{1,0:T(8,128)(2,1)}) custom-call(bf16[1024,512]{1,0:T(8,128)(2,1)} %bitcast.5, bf16[1024,512]{1,0:T(8,128)(2,1)} %get-tuple-element.10.h_ref, bf16[1024,512]{1,0:T(8,128)(2,1)} %bitcast.6, bf16[2,16,16,2,3,16,512]{6,5,4,3,2,1,0:T(8,128)(2,1)} %get-tuple-element.11.g_ref), custom_call_target="tpu_custom_call" | custom-call | tf_op jit(solution)/shard_map/backward_reduce/pallas_call | solution.py:511
  433.1 2.3 slice.3
  435.4 0.0 copy-start
  435.4 1.9 copy-done
  437.3 5.5 %restore_order.1 = (bf16[2,32,8192]{2,1,0:T(8,128)(2,1)}, bf16[2,32,8192]{2,1,0:T(8,128)(2,1)}) custom-call(bf16[2,16,3,32,512]{4,3,2,1,0:T(8,128)(2,1)S(1)} %copy-done), custom_call_target="tpu_custom_call" | custom-call | tf_op jit(solution)/shard_map/restore_order/pallas_call | solution.py:564
  442.8 2.3 copy.10
Async XLA Ops:
  435.4 1.9 copy-start

commit v2 on v0

v2 whole, which is shorter than its diff:
```python
import functools
import math

import jax
import jax.numpy as jnp
from jax import lax
from jax.experimental import pallas as pl
from jax.experimental.pallas import tpu as pltpu
from jax.sharding import PartitionSpec as P

F32, BF16 = jnp.float32, jnp.bfloat16
MESH = pl.DeviceIdType.MESH
LANES, PIECE = 128, 32
PER = LANES // PIECE
NN, NT, TN = ((1,), (0,)), ((1,), (1,)), ((0,), (0,))
SIGNS = (1, -1)
VMEM_LIMIT = 67_043_328


def dot(a, b, dims=NN):
    return lax.dot_general(a, b, (dims, ((), ())), preferred_element_type=F32)


def scale_of(wide):
    return lax.rsqrt(jnp.mean(wide**2, -1, keepdims=True) + 1e-6)


LEAD, GAP, AHEAD, DY = 0, 0, 4, 4


def place(n):
    side = math.isqrt(n)
    me = lax.axis_index("dp")
    x, y = me // side, lax.rem(me, side)

    def at(v, u, w):
        u, w = lax.rem(u + 2 * side, side), lax.rem(w + 2 * side, side)
        return u * side + w if v == 0 else w * side + u

    return me, side, ((x, y), (y, x)), at


def regroup(pieces, lane):
    for k in range(PER):
        out = pieces[k]
        for q in range(PER):
            if q != k:
                out = jnp.where(lane == q, pltpu.roll(pieces[q], (PIECE * (q - k)) % LANES, 1), out)
        yield k, out


def kernel(
    n, x_in, dy_in, wg_in, wu_in, wd_in, dx_out, dwg_out, dwu_out, dwd_out, g_ref,
    local, own, x_ref, h_ref, a_ref, at_ref, d_ref, shared, hid_ref, dg_ref, du_ref, dag, dau, w_buf, terms, mixed, result, result_down,
    sum_p, sum_q, swap_s, swap_r, raw_p_s, raw_p_r, run_p_s, run_p_r, raw_q_s, raw_q_r, run_q_s, run_q_r, turn_s, turn_r, last_s, last_r,
    in_sem, local_sem, down_sem, keep_sem, send_sem, recv_sem, pair_send, pair_recv, load_sem, out_sem, share_ss, share_rs,
    swap_ss, swap_rs, raw_p_ss, raw_p_rs, run_p_ss, run_p_rs, raw_q_ss, raw_q_rs, run_q_ss, run_q_rs, turn_ss, turn_rs, last_ss, last_rs,
):
    layers, chunks = g_ref.shape[:2]
    low, width = own.shape[3:]
    height, part = 2 * low, width // 2
    tokens, depth = x_ref.shape
    me, side, uw, at = place(n)
    x, y = uw[0]
    mate = x + 1 - 2 * lax.rem(x, 2)
    twin = lax.rem(x + 2 * lax.rem(x, 2) - 1 + side, side)
    twin_mate = twin + 1 - 2 * lax.rem(twin, 2)
    parity = lax.rem((x + 1) // 2, 2)
    rep = lax.axis_index("rep")
    core = lax.rem(rep, 2)
    partner = rep + 1 - 2 * core
    half = chunks // 2
    units = layers * half
    opening = half + 6 + GAP
    ahead, by_y = AHEAD * half // 8, DY * half // 8
    turnover = LEAD + half

    barrier = pltpu.get_barrier_semaphore()
    for s in SIGNS:
        pl.semaphore_signal(barrier, inc=1, device_id={"dp": at(0, x + s, y)}, device_id_type=MESH)
        pl.semaphore_signal(barrier, inc=1, device_id={"dp": at(0, x, y + s)}, device_id_type=MESH)
    pl.semaphore_signal(barrier, inc=1, device_id={"rep": partner}, device_id_type=MESH)


    first = pl.multiple_of(core * low, low)

    def fetch(layer, m):
        return pltpu.make_async_copy((wg_in, wu_in)[m].at[layer, pl.ds(first, low)], local.at[layer, m], local_sem.at[layer, m])

    def fetch_down(layer):
        return pltpu.make_async_copy(wd_in.at[layer, :, pl.ds(first, low)], own.at[layer, :, 2], down_sem.at[layer])

    inputs = [pltpu.make_async_copy(x_in, x_ref, in_sem.at[0]), pltpu.make_async_copy(dy_in, d_ref.at[pl.ds(0, tokens)], in_sem.at[1])]
    for layer in range(layers):
        for m in range(2):
            fetch(layer, m).start()
        fetch_down(layer).start()
    for copy in inputs:
        copy.start()

    lane_low = lax.broadcasted_iota(jnp.int32, (low, LANES), 1) // PIECE
    lane_high = lax.broadcasted_iota(jnp.int32, (height, LANES), 1) // PIECE
    per_device = wg_in.shape[2] // n
    tiles, groups = per_device // LANES, n // PER

    def columns(u, q, t):
        return pl.ds(pl.multiple_of((PER * u + q) * per_device + t * LANES, LANES), LANES)

    def tile_of(u):
        return pl.ds(pl.multiple_of(u * LANES, LANES), LANES)

    def keep(i):
        layer, some = i // tiles, pl.ds(PER * lax.rem(i, tiles), PER)
        return pltpu.make_async_copy(own.at[layer, some], g_ref.at[layer, some, me, core], keep_sem.at[i])

    def fill(i):
        layer, t = i // tiles, lax.rem(i, tiles)

        @pl.when(t == 0)
        def _():
            for m in range(2):
                fetch(layer, m).wait()
            fetch_down(layer).wait()

        def once(u, _):
            for m in range(2):
                pieces = [local[layer, m, :, columns(u, q, t)].astype(F32) for q in range(PER)]
                for k, out in regroup(pieces, lane_low):
                    own[layer, PER * t + k, m, :, tile_of(u)] = out.astype(BF16)
            return 0

        lax.fori_loop(0, groups, once, 0)
        keep(i).start()


    def place_of(k, v):
        return k // half, 2 * lax.rem(k, half) + v

    def block(k, v, d):
        layer, j = place_of(k, v)
        return g_ref.at[layer, j, d, core]

    def copy_to(k, v, d, device, src=None):
        return pltpu.make_async_remote_copy(
            src_ref=block(k, v, d) if src is None else src,
            dst_ref=block(k, v, d),
            send_sem=send_sem,
            recv_sem=recv_sem.at[k, v, d],
            device_id={"dp": device},
            device_id_type=MESH,
        )

    def await_block(k, v, d):
        copy_to(k, v, d, me).wait_recv()

    def begin(k):
        for v, (u, w) in enumerate(uw):
            layer, j = place_of(k, v)
            for s in SIGNS:
                copy_to(k, v, me, at(v, u + s, w), own.at[layer, j]).start()
                copy_to(k, v, me, at(v, u, w + s), own.at[layer, j]).start()

    def spread(k, v, d, u, w):
        for s in SIGNS:
            copy_to(k, v, d, at(v, u, w + s)).start()

    def pass_on(k, v, column, sign):
        u, w = uw[v]
        for s in SIGNS:
            await_block(k, v, at(v, u + column, w + s))
        copy_to(k, v, at(v, u + column, w - sign), at(v, u, w + sign)).start()

    def ways(k):
        sign, later = 1 - 2 * lax.rem(k, 2), k // half
        across = (2 * lax.rem(x, 2) - 1) * (1 - 2 * later)
        return across, sign, across, -sign

    def near(k):
        signs = ways(k)
        for v, (u, w) in enumerate(uw):
            for s in SIGNS:
                await_block(k, v, at(v, u + s, w))
            copy_to(k, v, at(v, u - signs[v], w), at(v, u + signs[v], w)).start()
            for s in SIGNS:
                spread(k, v, at(v, u + s, w), u, w)
            pass_on(k, v, 0, signs[1 - v])

    def middle(k):
        signs = ways(k)
        for v, (u, w) in enumerate(uw):
            await_block(k, v, at(v, u + 2, w))
            spread(k, v, at(v, u + 2, w), u, w)
            pass_on(k, v, 1, signs[3 - v])
            pass_on(k, v, -1, signs[1 - v])

    def far(k):
        signs = ways(k)
        for v, (u, w) in enumerate(uw):
            pass_on(k, v, 2, signs[3 - v])
            await_block(k, v, at(v, u, w + 2))

    def pair_copy(k, whose):
        layer, j = place_of(k, 0)
        ref = g_ref.at[layer, pl.ds(j, 2), :, whose]
        return pltpu.make_async_remote_copy(
            src_ref=ref, dst_ref=ref, send_sem=pair_send, recv_sem=pair_recv.at[k], device_id={"rep": partner}, device_id_type=MESH
        )

    def last(k):
        for v, (u, w) in enumerate(uw):
            for column in (1, -1, 2):
                await_block(k, v, at(v, u + column, w + 2))

        @pl.when(lax.rem(k, PER // 2) == 0)
        def _():
            keep(k // (PER // 2)).wait()

        pair_copy(k, core).start()


    def load(layer, j, slot):
        return pltpu.make_async_copy(g_ref.at[layer, j], w_buf.at[slot], load_sem.at[slot])

    def load_unit(k, v):
        return load(0, 2 * k + v, 2 * lax.rem(k, 2) + v)

    def load_other(o):
        return load(layers - 1 - o // half, 2 * lax.rem(o, half) + 1 - parity, lax.rem(o, 2))

    def load_mine(c):
        return load(layers - 1 - c // half, 2 * lax.rem(c, half) + parity, 2 + lax.rem(c, 2))

    def both(k):
        pair_copy(k, 1 - core).wait_recv()

        @pl.when(k < half)
        def _():
            for v in range(2):
                load_unit(k, v).start()

    mine_rows, mate_rows = pl.ds(0, tokens), pl.ds(tokens, tokens)

    def matrices(slot):
        return [w_buf[slot, :, :, m].reshape(depth, width) for m in range(3)]

    def sigmoid(z):
        return 0.5 * jnp.tanh(0.5 * z) + 0.5

    def forward(k):
        for rows, total in ((mine_rows, dag), (mate_rows, dau)):
            if rows is mate_rows:

                @pl.when(k == 0)
                def _():
                    share_all(0).wait_recv()
                    wide = shared[0].astype(F32)
                    a_ref[mate_rows] = (wide * scale_of(wide)).astype(BF16)

            for v in range(2):
                if rows is mine_rows:
                    load_unit(k, v).wait()
                wg, wu, wd = matrices(2 * lax.rem(k, 2) + v)
                a = a_ref[rows]
                gate, up = dot(a, wg), dot(a, wu)
                total[...] += dot((gate * sigmoid(gate) * up).astype(BF16), wd)


    def share(kind, piece, count=1):
        rows = pl.ds(piece * (tokens // half), count * (tokens // half))
        source = (x_ref, h_ref, d_ref, d_ref)[kind]
        return pltpu.make_async_remote_copy(
            src_ref=source.at[rows],
            dst_ref=shared.at[kind, rows],
            send_sem=share_ss.at[kind],
            recv_sem=share_rs.at[kind],
            device_id={"dp": at(0, mate, y)},
            device_id_type=MESH,
        )

    def share_all(kind):
        return share(kind, 0, half)


    def normed(source, rows):
        wide = source.astype(F32)
        a = wide * scale_of(wide)
        a_ref[rows] = a.astype(BF16)
        at_ref[:, rows] = a.T.astype(BF16)

    def start_layer(source):
        normed(source[...], mine_rows)
        dag[...] = jnp.zeros_like(dag)
        dau[...] = jnp.zeros_like(dau)

    def meet(kind, by_kind):
        normed(shared[kind], mate_rows)
        share_all(by_kind).wait_recv()
        d_ref[mate_rows] = shared[by_kind]

    def end_layer(source):
        wide = source[...].astype(F32)
        scale = scale_of(wide)
        da = (dag[...].astype(BF16) + dau[...].astype(BF16)).astype(F32)
        inner = jnp.sum(da * wide, -1, keepdims=True)
        by_h = da * scale - wide * (scale * scale * scale * inner / depth)
        d_ref[mine_rows] = d_ref[mine_rows] + by_h.astype(BF16)

    def by_hidden(slot, rows, kept):
        wg, wu, wd = matrices(slot)
        a, d = a_ref[rows], d_ref[rows]
        gate, up = dot(a, wg), dot(a, wu)
        by_hid = dot(d, wd, NT).astype(BF16).astype(F32)
        sig = sigmoid(gate)
        silu = gate * sig
        dg = (by_hid * up * (sig + silu * (1 - sig))).astype(BF16)
        du = (by_hid * silu).astype(BF16)
        if kept:
            hid_ref[rows] = (silu * up).astype(BF16)
            dg_ref[rows] = dg
            du_ref[rows] = du
        return dg, du, wg, wu

    def own_part(slot, kept):
        dg, du, wg, wu = by_hidden(slot, mine_rows, kept)
        dag[...] += dot(dg, wg, NT)
        dau[...] += dot(du, wu, NT)

    def compute(c):
        held, slot = lax.rem(c, 3), 2 + lax.rem(c, 2)
        load_mine(c).wait()
        own_part(slot, True)
        by_hidden(slot, mate_rows, True)
        step = n // 2
        for m, (left, right, dims) in enumerate(((at_ref, dg_ref, NN), (at_ref, du_ref, NN), (hid_ref, d_ref, TN))):
            for i in range(2):
                some = pl.ds(i * step * height, step * height)
                value = dot(left[some] if dims is NN else left[:, some], right[...], dims)
                terms[held, m, i * step : (i + 1) * step] = value.reshape(step, height, width)


    P_ROWS, Q_ROWS = slice(0, low), slice(low, height)
    MINE, THEIRS = (x, mate), (twin, twin_mate)

    def cols_of(h):
        return slice(h * part, (h + 1) * part)

    def remote(k, src, dst, src_sem, dst_sem, device, *index):
        return pltpu.make_async_remote_copy(
            src_ref=src.at[(lax.rem(k, 2), *index)],
            dst_ref=dst.at[(lax.rem(k, 4), *index)],
            send_sem=src_sem.at[(lax.rem(k, 2), *index)],
            recv_sem=dst_sem.at[(lax.rem(k, 4), *index)],
            device_id={"dp": device},
            device_id_type=MESH,
        )

    def down_the_column(src, dst, src_sem, dst_sem):
        return lambda k: [remote(k, src, dst, src_sem, dst_sem, at(0, x, y + s), i) for i, s in enumerate(SIGNS)]

    swap = lambda k: [remote(k, swap_s, swap_r, swap_ss, swap_rs, at(0, twin, y))]
    turn = lambda k: [remote(k, turn_s, turn_r, turn_ss, turn_rs, at(0, twin, y))]
    hand = lambda k: [remote(k, last_s, last_r, last_ss, last_rs, at(0, mate, y))]
    raw_p = down_the_column(raw_p_s, raw_p_r, raw_p_ss, raw_p_rs)
    run_p = down_the_column(run_p_s, run_p_r, run_p_ss, run_p_rs)
    raw_q = down_the_column(raw_q_s, raw_q_r, raw_q_ss, raw_q_rs)
    run_q = down_the_column(run_q_s, run_q_r, run_q_ss, run_q_rs)

    def go(copies):
        for copy in copies:
            copy.start()

    def arrive(copies):
        for copy in copies:
            copy.wait()

    def row(w):
        return lax.rem(w + 2 * side, side)

    def slots(k):
        return lax.rem(k, 3), lax.rem(k, 2), lax.rem(k, 4)

    def pack(c):
        held, slot, _ = slots(c)
        for e, column in enumerate(THEIRS):
            for w in range(side):
                swap_s[slot, e, w] = terms[held, :, at(0, column, w), P_ROWS].astype(BF16)
        go(swap(c))
        for i, s in enumerate(SIGNS):
            for u in range(side):
                raw_q_s[slot, i, 0, u] = terms[held, :, at(0, u, y + 2), Q_ROWS, cols_of(i)].astype(BF16)
                raw_q_s[slot, i, 1, u] = terms[held, :, at(0, u, y + s), Q_ROWS, cols_of(1 - i)].astype(BF16)
        go(raw_q(c))

    def stage1(c):
        held, slot, got = slots(c)
        arrive(swap(c))
        for e, column in enumerate(MINE):
            for w in range(side):
                sum_p[slot, e, w] = terms[held, :, at(0, column, w), P_ROWS] + swap_r[got, e, w].astype(F32)
        for i, s in enumerate(SIGNS):
            for e in range(2):
                raw_p_s[slot, i, 0, e] = sum_p[slot, e, row(y + 2), :, :, cols_of(i)].astype(BF16)
                raw_p_s[slot, i, 1, e] = sum_p[slot, e, row(y + s), :, :, cols_of(1 - i)].astype(BF16)
        go(raw_p(c))
        arrive(raw_q(c))
        for i, s in enumerate(SIGNS):
            for u in range(side):
                value = terms[held, :, at(0, u, y + s), Q_ROWS, cols_of(i)] + raw_q_r[got, i, 0, u].astype(F32)
                run_q_s[slot, i, u] = value.astype(BF16)
        go(run_q(c))

    def stage2(c):
        held, slot, got = slots(c)
        arrive(raw_p(c))
        for i, s in enumerate(SIGNS):
            for e in range(2):
                value = sum_p[slot, e, row(y + s), :, :, cols_of(i)] + raw_p_r[got, i, 0, e].astype(F32)
                run_p_s[slot, i, e] = value.astype(BF16)
        go(run_p(c))
        arrive(run_q(c))
        for i in range(2):
            for e in range(2):
                for column, mine in ((MINE[e], True), (THEIRS[e], False)):
                    value = terms[held, :, at(0, column, y), Q_ROWS, cols_of(i)]
                    value = value + run_q_r[got, i, column].astype(F32) + raw_q_r[got, 1 - i, 1, column].astype(F32)
                    if mine:
                        sum_q[slot, e, :, :, cols_of(i)] = value
                    else:
                        turn_s[slot, e, :, :, cols_of(i)] = value.astype(BF16)
        go(turn(c))

    def own_chunk(c, other):
        return layers - 1 - c // half, 2 * lax.rem(c, half) + (1 - parity if other else parity)

    def settle(c, value, rows, cols):
        layer, j = own_chunk(c, False)
        mixed[:, lax.rem(j, PER), rows, cols] = value[:2]
        result_down[layer, j, rows, cols] = value[2]

    def stage3(c):
        held, slot, got = slots(c)
        arrive(run_p(c))
        for i in range(2):
            for e in range(2):
                value = sum_p[slot, e, y, :, :, cols_of(i)] + run_p_r[got, i, e].astype(F32) + raw_p_r[got, 1 - i, 1, e].astype(F32)
                if e == 0:
                    settle(c, value.astype(BF16), P_ROWS, cols_of(i))
                else:
                    last_s[slot, :, P_ROWS, cols_of(i)] = value.astype(BF16)
        arrive(turn(c))
        for e in range(2):
            value = (sum_q[slot, e] + turn_r[got, e].astype(F32)).astype(BF16)
            if e == 0:
                settle(c, value, Q_ROWS, slice(0, width))
            else:
                last_s[slot, :, Q_ROWS] = value
        go(hand(c))

    def put(layer):
        return [
            pltpu.make_async_copy(src.at[layer], dst.at[layer], out_sem.at[layer, m])
            for m, (src, dst) in enumerate(((result.at[0], dwg_out), (result.at[1], dwu_out), (result_down, dwd_out)))
        ]

    def stage4(c):
        _, _, got = slots(c)
        layer, j = own_chunk(c, True)
        arrive(hand(c))
        mixed[:, lax.rem(j, PER)] = last_r[got, :2]
        result_down[layer, j] = last_r[got, 2]

        @pl.when(lax.rem(c, PER // 2) == PER // 2 - 1)
        def _():
            def once(u, _):
                for m in range(2):
                    pieces = [mixed[m, q, :, tile_of(u)].astype(F32) for q in range(PER)]
                    for q, out in regroup(pieces, lane_high):
                        result[m, layer, :, columns(u, q, j // PER)] = out.astype(BF16)
                return 0

            lax.fori_loop(0, groups, once, 0)

        @pl.when(lax.rem(c, half) == half - 1)
        def _():
            for copy in put(layer):
                copy.start()

    def unit_at(t):
        q = t // (half + GAP)
        return t - GAP * q, (t >= 0) & (t < 2 * half + GAP) & (t - q * (half + GAP) < half)

    def mine_at(r):
        r = r - LEAD
        q = (r + 1024 - half - ahead) // 1024
        c = r - q * ahead
        return c, (r >= 0) & (r - q * (half + ahead) < half), (r >= 0) & ((r < half) | (q == 1))

    def other_at(r):
        late = r - turnover
        q = late // (half + ahead)
        return (r, (r >= 0) & (r < half)), (half + late - q * half, ((late >= 0) & (late < ahead)) | ((late >= half + ahead) & (late < 2 * half)))

    fill(0)
    pl.semaphore_wait(barrier, 5)

    def stages_at(t, *stages):
        for lag, stage in stages:
            k, here = unit_at(t - lag)

            @pl.when((t >= lag) & here)
            def _(k=k, stage=stage):
                stage(k)

    def step(t, _):
        r = t - opening
        (o, early), (o_late, late) = other_at(r)
        (o_soon, soon), (o_next, next_late) = other_at(r + 1)
        c, mine, going = mine_at(r)
        c_next, mine_next, _ = mine_at(r + 1)

        @pl.when(r == turnover)
        def _():
            share_all(2).wait_send()
            end_layer(h_ref)
            start_layer(x_ref)
            share_all(3).start()

        @pl.when(mine_next & (c_next >= half))
        def _():
            load_mine(c_next).start()

        for lag, stage in ((5, stage4), (4, stage3), (3, stage2), (2, stage1)):

            @pl.when(going & (c >= lag) & (c - lag < 2 * half))
            def _(lag=lag, stage=stage):
                stage(c - lag)

        @pl.when(next_late)
        def _():
            load_other(o_next).start()

        @pl.when(early | late)
        def _():
            chunk = o - (o - o_late) * ((r + 2 * half) // (turnover + 2 * half))
            load_other(chunk).wait()
            own_part(lax.rem(chunk, 2), False)

        stages_at(t, (5, both), (0, begin), (1, near), (2, middle), (3, far), (4, last))

        @pl.when(mine_next & (c_next < half))
        def _():
            load_mine(c_next).start()

        @pl.when(soon)
        def _():
            load_other(o_soon).start()

        coming, here = unit_at(t + 1)

        @pl.when(here & (lax.rem(coming, PER // 2) == 0))
        def _():
            fill(coming // (PER // 2))

        @pl.when(t == 0)
        def _():
            for copy in inputs:
                copy.wait()
            wide = x_ref[...].astype(F32)
            a_ref[mine_rows] = (wide * scale_of(wide)).astype(BF16)
            dag[...] = jnp.zeros_like(dag)
            dau[...] = jnp.zeros_like(dau)

        @pl.when(t < half // 2)
        def _():
            share(0, 2 * t, 2).start()

        @pl.when((t >= by_y) & (t < by_y + half))
        def _():
            share(2, t - by_y).start()

        @pl.when((t >= 5) & (t < half + 5))
        def _():
            forward(t - 5)

        @pl.when(t == half + 4)
        def _():
            h_ref[...] = x_ref[...] + dag[...].astype(BF16)
            shared[1] = shared[0] + dau[...].astype(BF16)
            start_layer(h_ref)

        @pl.when(r == LEAD)
        def _():
            meet(1, 2)

        @pl.when(r == turnover + ahead)
        def _():
            meet(0, 3)

        @pl.when((r >= LEAD) & mine)
        def _():
            compute(c)
            pack(c)

        @pl.when(r == turnover + 2 * half)
        def _():
            share_all(3).wait_send()
            end_layer(x_ref)
            pltpu.make_async_copy(d_ref.at[mine_rows], dx_out, in_sem.at[0]).start()

        return 0

    lax.fori_loop(0, opening + turnover + max(2 * half + 1, ahead + half + 5), step, 0)
    share_all(0).wait_send()
    pltpu.make_async_copy(d_ref.at[mine_rows], dx_out, in_sem.at[0]).wait()
    for layer in range(layers):
        for copy in put(layer):
            copy.wait()
    for sem, blocks in ((send_sem, n - 1), (pair_send, n)):
        ref = g_ref.at[:, :, pl.ds(0, blocks), 0]
        pltpu.make_async_copy(ref, ref, sem).wait()


def copy_kernel(*refs):
    count = (len(refs) - 2) // 3
    given, got, held, (in_sem, out_sem) = refs[:count], refs[count : 2 * count], refs[2 * count : 3 * count], refs[3 * count :]
    come = [pltpu.make_async_copy(a, b, in_sem.at[i]) for i, (a, b) in enumerate(zip(given, held, strict=True))]
    leave = [pltpu.make_async_copy(a, b, out_sem.at[i]) for i, (a, b) in enumerate(zip(held, got, strict=True))]
    for copy in come:
        copy.start()
    for first, second in zip(come, leave, strict=True):
        first.wait()
        second.start()
    for copy in leave:
        copy.wait()


def copied(*arrays):
    anywhere = pl.BlockSpec(memory_space=pl.ANY)
    return pl.pallas_call(
        copy_kernel,
        out_shape=[jax.ShapeDtypeStruct(a.shape, a.dtype) for a in arrays],
        in_specs=[anywhere] * len(arrays),
        out_specs=[anywhere] * len(arrays),
        scratch_shapes=[*[pltpu.VMEM(a.shape, a.dtype) for a in arrays], *[pltpu.SemaphoreType.DMA((len(arrays),))] * 2],
        compiler_params=pltpu.CompilerParams(vmem_limit_bytes=VMEM_LIMIT),
        name="copied",
    )(*arrays)


def run(n, x, dy, wg, wu, wd):
    (layers, height, local_width), (tokens, depth) = wg.shape, x.shape
    width = n * PIECE
    chunks = wd.shape[1] // PIECE
    assert depth == width and height == PIECE and layers == 2
    low, side, part = height // 2, math.isqrt(n), width // 2
    anywhere = pl.BlockSpec(memory_space=pl.ANY)
    sems = lambda *counts: pltpu.SemaphoreType.DMA(counts)
    bf16, f32 = (lambda *dims: pltpu.VMEM(dims, BF16)), (lambda *dims: pltpu.VMEM(dims, F32))
    whole, block = (3, low, width), (3, low, part)
    piece = (n, 2, 3, low, width)
    shape = lambda *dims: jax.ShapeDtypeStruct(dims, BF16)
    down = (layers, chunks, PIECE, depth)
    slots = lambda *dims: [bf16(2, *dims), bf16(4, *dims)]
    *results, _ = pl.pallas_call(
        functools.partial(kernel, n),
        out_shape=(shape(*x.shape), shape(*wg.shape), shape(*wu.shape), shape(*down), shape(layers, chunks, *piece)),
        in_specs=[anywhere] * 5,
        out_specs=(anywhere,) * 5,
        scratch_shapes=[
            bf16(layers, 2, low, local_width),
            bf16(layers, chunks, *whole),
            *[bf16(*x.shape)] * 2,
            bf16(2 * tokens, depth), bf16(depth, 2 * tokens), bf16(2 * tokens, depth),
            bf16(4, tokens, depth),
            *[bf16(2 * tokens, width)] * 3,
            *[f32(*x.shape)] * 2,
            bf16(4, *piece),
            f32(3, 3, n, height, width),
            bf16(2, PER, height, width), bf16(2, *wg.shape), bf16(*down),
            f32(2, 2, side, *whole), f32(2, 2, *whole),
            *slots(2, side, *whole),
            *slots(2, 2, 2, *block), *slots(2, 2, *block),
            *slots(2, 2, side, *block), *slots(2, side, *block),
            *slots(2, *whole), *slots(3, height, width),
            sems(2), sems(layers, 2), sems(layers), sems(layers * chunks // PER),
            pltpu.SemaphoreType.DMA, sems(layers * chunks // 2, 2, n), pltpu.SemaphoreType.DMA, sems(layers * chunks // 2),
            sems(4), sems(layers, 3), sems(4), sems(4),
            sems(2), sems(4), *[sems(2, 2), sems(4, 2)] * 4, *[sems(2), sems(4)] * 2,
        ],
        compiler_params=pltpu.CompilerParams(collective_id=0, has_side_effects=True, vmem_limit_bytes=VMEM_LIMIT),
        name="layers",
    )(x, dy, wg, wu, wd.reshape(down))
    dx, dwg, dwu, dwd = copied(*results)
    return dx, dwg, dwu, dwd.reshape(wd.shape)


def solution(mesh):
    n = mesh.shape["dp"]

    def step(x, dy, wg, wu, wd):
        dx, *by_weights = run(n, x[0], dy[0], wg, wu, wd)
        return (dx[None], *by_weights)

    tokens, rows, out = P(("rep", "dp"), None, None), P(None, "dp", None), P("rep", "dp", None)
    return jax.shard_map(step, mesh=mesh, in_specs=(tokens, tokens, rows, rows, rows), out_specs=(tokens, out, out, out), check_vma=False)
```

time: 1180 us -> 391 us (0.33)
  waiting for transfers between devices: 713 us -> 0 us
  Pallas kernels: 0 us -> 384 us
  matrix products: 318 us -> 0 us
  other arithmetic: 97.3 us -> 0 us
  local copies, waits for them, and re-layouts: 25.6 us -> 0 us
  between operations: 14.9 us -> 0.64 us
    unnamed x18 -> x0, waiting for transfers between devices: 437 us -> none
    pallas_call x0 -> x2, Pallas kernels: none -> 384 us  [the longest x1 381 us: run(): pl.pallas_call(functools.partial(kernel, n), out_shape=(shape(*x.shape),...]
    dot_general x17 -> x0, matrix products: 318 us -> none  [the longest x6 132 us: layer(): up = jnp.dot(a, w['w_up'], preferred_element_type=jnp.float32)]
    squeeze x6 -> x0, waiting for transfers between devices: 276 us -> none  [stack(): h = layer(h, {name: w[number] for name, w in weights.items()})]
    unnamed x3 -> x0, other arithmetic: 81.7 us -> none
    unnamed x31 -> x0, local copies, waits for them, and re-layouts: 18.8 us -> none
  transfers between devices with their start and end apart: 12 -> 0, of which waited for: 11 -> 0; matrix products, arithmetic and copies ran while one was open for 28% -> 0% of each run, Pallas kernels for 0% -> 0%
where the time goes in v2:
time: 391 us; the launch traced here: 385 us
  Pallas kernels  384 us (98%)
    pallas_call x1, Pallas kernels, run(): pl.pallas_call(functools.partial(kernel, n), out_shape=(shape(*x.shape),...  381 us

profile of v2, /device:TPU:97, one launch (start us, length us, event | category | flops | bytes accessed | tf_op | source)
XLA Modules:
  0.0 384.8 jit_solution(10716667767847046293)
XLA Ops:
  0.6 380.9 %layers.1 = (bf16[1024,512]{1,0:T(8,128)(2,1)}, bf16[2,32,8192]{2,1,0:T(8,128)(2,1)}, bf16[2,32,8192]{2,1,0:T(8,128)(2,1)}, bf16[2,16,32,512]{3,2,1,0:T(8,128)(2,1)}, bf16[2,16,16,2,3,16,512]{6,5,4,3,2,1,0:T(8,128)(2,1)}) custom-call(bf16[1024,512]{1,0:T(8,128)(2,1)} %bitcast.5, bf16[1024,512]{1,0:T(8,128)(2,1)} %bitcast.6, bf16[2,32,8192]{2,1,0:T(8,128)(2,1)} %wg_in.1, ...), custom_call_target="tpu_custom_call" | custom-call | tf_op jit(solution)/shard_map/layers/pallas_call | solution.py:664
  381.5 3.3 copied.1

commit v3 on v2

--- a/solution.py
+++ b/solution.py
@@ -25,7 +25,7 @@
     return lax.rsqrt(jnp.mean(wide**2, -1, keepdims=True) + 1e-6)
 
 
-LEAD, GAP, AHEAD, DY = 0, 0, 4, 4
+LEAD, GAP, AHEAD, DY = 0, 0, 5, 6
 
 
 def place(n):
@@ -171,9 +171,10 @@
         copy_to(k, v, at(v, u + column, w - sign), at(v, u, w + sign)).start()
 
     def ways(k):
-        sign, later = 1 - 2 * lax.rem(k, 2), k // half
+        sign, later = 1 - 2 * lax.rem(k, 2), k // (half + 3 * half // 4)
         across = (2 * lax.rem(x, 2) - 1) * (1 - 2 * later)
-        return across, sign, across, -sign
+        first = 1 - (k + units - half // 2) // units
+        return across, sign, sign + (across - sign) * (later + first), -sign
 
     def near(k):
         signs = ways(k)
@@ -246,23 +247,14 @@
     def sigmoid(z):
         return 0.5 * jnp.tanh(0.5 * z) + 0.5
 
-    def forward(k):
-        for rows, total in ((mine_rows, dag), (mate_rows, dau)):
-            if rows is mate_rows:
-
-                @pl.when(k == 0)
-                def _():
-                    share_all(0).wait_recv()
-                    wide = shared[0].astype(F32)
-                    a_ref[mate_rows] = (wide * scale_of(wide)).astype(BF16)
-
-            for v in range(2):
-                if rows is mine_rows:
-                    load_unit(k, v).wait()
-                wg, wu, wd = matrices(2 * lax.rem(k, 2) + v)
-                a = a_ref[rows]
-                gate, up = dot(a, wg), dot(a, wu)
-                total[...] += dot((gate * sigmoid(gate) * up).astype(BF16), wd)
+    def forward(k, rows, total):
+        for v in range(2):
+            if rows is mine_rows:
+                load_unit(k, v).wait()
+            wg, wu, wd = matrices(2 * lax.rem(k, 2) + v)
+            a = a_ref[rows]
+            gate, up = dot(a, wg), dot(a, wu)
+            total[...] += dot((gate * sigmoid(gate) * up).astype(BF16), wd)
 
 
     def share(kind, piece, count=1):
@@ -290,7 +282,6 @@
     def start_layer(source):
         normed(source[...], mine_rows)
         dag[...] = jnp.zeros_like(dag)
-        dau[...] = jnp.zeros_like(dau)
 
     def meet(kind, by_kind):
         normed(shared[kind], mate_rows)
@@ -330,9 +321,9 @@
         load_mine(c).wait()
         own_part(slot, True)
         by_hidden(slot, mate_rows, True)
-        step = n // 2
+        step = n
         for m, (left, right, dims) in enumerate(((at_ref, dg_ref, NN), (at_ref, du_ref, NN), (hid_ref, d_ref, TN))):
-            for i in range(2):
+            for i in range(1):
                 some = pl.ds(i * step * height, step * height)
                 value = dot(left[some] if dims is NN else left[:, some], right[...], dims)
                 terms[held, m, i * step : (i + 1) * step] = value.reshape(step, height, width)
@@ -522,8 +513,9 @@
         def _():
             share_all(2).wait_send()
             end_layer(h_ref)
+            share_all(3).start()
             start_layer(x_ref)
-            share_all(3).start()
+            dau[...] = jnp.zeros_like(dau)
 
         @pl.when(mine_next & (c_next >= half))
         def _():
@@ -547,7 +539,7 @@
 
         stages_at(t, (5, both), (0, begin), (1, near), (2, middle), (3, far), (4, last))
 
-        @pl.when(mine_next & (c_next < half))
+        @pl.when(mine_next & (c_next < half) & (c_next > 0))
         def _():
             load_mine(c_next).start()
 
@@ -570,9 +562,13 @@
             dag[...] = jnp.zeros_like(dag)
             dau[...] = jnp.zeros_like(dau)
 
-        @pl.when(t < half // 2)
-        def _():
-            share(0, 2 * t, 2).start()
+        @pl.when((t < 6) & (t + t // 3 < half))
+        def _():
+            share(0, t + t // 3).start()
+
+        @pl.when((lax.rem(t, 3) == 2) & (t + t // 3 + 1 < half))
+        def _():
+            share(0, t + t // 3 + 1).start()
 
         @pl.when((t >= by_y) & (t < by_y + half))
         def _():
@@ -580,13 +576,28 @@
 
         @pl.when((t >= 5) & (t < half + 5))
         def _():
-            forward(t - 5)
+            forward(t - 5, mine_rows, dag)
+
+        @pl.when(t == 6)
+        def _():
+            share_all(0).wait_recv()
+            wide = shared[0].astype(F32)
+            a_ref[mate_rows] = (wide * scale_of(wide)).astype(BF16)
+
+        @pl.when((t >= 6) & (t < half + 6))
+        def _():
+            forward(t - 6, mate_rows, dau)
 
         @pl.when(t == half + 4)
         def _():
             h_ref[...] = x_ref[...] + dag[...].astype(BF16)
+            start_layer(h_ref)
+
+        @pl.when(t == half + 5)
+        def _():
             shared[1] = shared[0] + dau[...].astype(BF16)
-            start_layer(h_ref)
+            dau[...] = jnp.zeros_like(dau)
+            load_mine(0).start()
 
         @pl.when(r == LEAD)
         def _():

time: 391 us -> 373 us (0.954)
  Pallas kernels: 384 us -> 369 us
    pallas_call x1, Pallas kernels: 381 us -> 366 us  [run(): pl.pallas_call(functools.partial(kernel, n), out_shape=(shape(*x.shape),...]
where the time goes in v3:
time: 373 us; the launch traced here: 370 us
  Pallas kernels  369 us (99%)
    pallas_call x1, Pallas kernels, run(): pl.pallas_call(functools.partial(kernel, n), out_shape=(shape(*x.shape),...  366 us

profile of v3, /device:TPU:97, one launch (start us, length us, event | category | flops | bytes accessed | tf_op | source)
XLA Modules:
  0.0 370.0 jit_solution(7635990415934291329)
XLA Ops:
  0.6 366.0 %layers.1 = (bf16[1024,512]{1,0:T(8,128)(2,1)}, bf16[2,32,8192]{2,1,0:T(8,128)(2,1)}, bf16[2,32,8192]{2,1,0:T(8,128)(2,1)}, bf16[2,16,32,512]{3,2,1,0:T(8,128)(2,1)}, bf16[2,16,16,2,3,16,512]{6,5,4,3,2,1,0:T(8,128)(2,1)}) custom-call(bf16[1024,512]{1,0:T(8,128)(2,1)} %bitcast.5, bf16[1024,512]{1,0:T(8,128)(2,1)} %bitcast.6, bf16[2,32,8192]{2,1,0:T(8,128)(2,1)} %wg_in.1, ...), custom_call_target="tpu_custom_call" | custom-call | tf_op jit(solution)/shard_map/layers/pallas_call | solution.py:675
  366.7 3.3 copied.1
